TPU v7x, 256 devices: a whole 4x4x8 slice. The times are simulated.
256 devices in a mesh: ctx: 64 (over x, z_hi, y, core), tp: 4 (over z_lo).
Axes of the slice: x: 4, y: 4, z: 8 (z_hi: 2, z_lo: 4; z = z_hi * 4 + z_lo), core: 2. Of those that a mesh axis runs over, the one named last changes fastest.
Arguments:
- queries: bfloat16 [8192, 32, 128], P('ctx', 'tp'), may hold values from -8 to 8
- window_keys: bfloat16 [8192, 4, 128], P('ctx', 'tp'), may hold values from -8 to 8
- window_values: bfloat16 [8192, 4, 128], P('ctx', 'tp'), may hold values from -6 to 6
- anchor_keys: bfloat16 [4096, 4, 128], P('ctx', 'tp'), may hold values from -8 to 8
- anchor_values: bfloat16 [4096, 4, 128], P('ctx', 'tp'), may hold values from -6 to 6
- passing_rows: int32 [64, 32], replicated, may hold values from 0 to 127, as said below
- block_of_device: int32 [64], replicated, may hold values from 0 to 63, each once
- out_weight: bfloat16 [4096, 4096], P(None, 'tp'), may hold values from -0.09375 to 0.09375
Outputs:
- mixed: bfloat16 [4096, 8192], P('tp', 'ctx')
Inputs may be any that keep to these rules, and one draw needn't show every extreme that they name: `passing_rows`: each row holds 32 different positions. `block_of_device`: every block number appears once.
All inputs are finite; a program needn't handle non-finite values.
Results may differ from a plain program's by a relative error of at most 0.013.
Values may be sent and summed in bfloat16 or wider, within the bound.
A program may use at most 128 MiB of HBM per device.

v0:
```python
import jax
import jax.numpy as jnp
from jax import lax
from jax.sharding import Mesh
from jax.sharding import PartitionSpec as P

CTX = ("ctx_0", "ctx_1", "ctx_2", "ctx_3")


def copy_for_each(array, axis):
    size = lax.axis_size(axis)
    return lax.all_to_all(
        jnp.broadcast_to(array[None], (size, *array.shape)), axis, 0, 0, tiled=True
    )


def joined_along(parts, dim):
    parts = jnp.moveaxis(parts, 0, dim)
    lengths = parts.shape
    return parts.reshape(*lengths[:dim], lengths[dim] * lengths[dim + 1], *lengths[dim + 2 :])


def gathered_by_axis(array, axes, dim):
    far, near = axes
    leading = copy_for_each(array, far)
    parts = jnp.swapaxes(copy_for_each(leading, near), 0, 1)
    return joined_along(parts.reshape(-1, *array.shape), dim)


def side_by_side(arrays, axis, dim, along):
    widths = [a.shape[along] for a in arrays]
    both = jnp.concatenate(arrays, axis=along)
    filled = gathered_by_axis(both, axis, dim)
    return tuple(jnp.split(filled, [sum(widths[:k]) for k in range(1, len(widths))], axis=along))


def side_by_side_2(arrays, axis, dim, along):
    widths = [a.shape[along] for a in arrays]
    both = jnp.concatenate(arrays, axis=along)
    filled = lax.all_gather(both, axis, axis=dim, tiled=True)
    return tuple(jnp.split(filled, [sum(widths[:k]) for k in range(1, len(widths))], axis=along))


def in_blocks(array, dim, size):
    lengths = array.shape
    parts = array.reshape(*lengths[:dim], size, lengths[dim] // size, *lengths[dim + 1 :])
    return jnp.moveaxis(parts, dim, 0)


def sent_and_summed(array, axis, dim):
    parts = in_blocks(array, dim, lax.axis_size(axis))
    arrived = lax.all_to_all(parts, axis, split_axis=0, concat_axis=0, tiled=True)
    return arrived.astype(jnp.float32).sum(axis=0)


def lookup(lookup_table, slot_ids):
    matches = slot_ids[:, None] == jnp.arange(lookup_table.shape[0], dtype=jnp.int32)[None, :]
    return jnp.sum(jnp.where(matches, lookup_table[None, :], 0), axis=1)


def attend(fold_state, grouped, key_rows, value_rows, visible):
    running_max, running_sum, weighted = fold_state
    key_count = key_rows.shape[0]
    score_scale = grouped.shape[-1] ** (-0.5)
    for first_key in range(0, key_count, 1024):
        last_key = min(first_key + 1024, key_count)
        visible_part = visible[:, first_key:last_key][:, None, None, :]
        scores = (
            jnp.einsum(
                "tgjd,ngd->tgjn",
                grouped,
                key_rows[first_key:last_key],
                preferred_element_type=jnp.float32,
            )
            * score_scale
        )
        scores = jnp.where(visible_part, scores, -1e30)
        new_max = jnp.maximum(running_max, jnp.max(scores, axis=-1))
        weights = jnp.where(visible_part, jnp.exp(scores - new_max[..., None]), 0.0)
        factor = jnp.exp(running_max - new_max)
        running_sum = running_sum * factor + jnp.sum(weights, axis=-1)
        weighted = weighted * factor[..., None] + jnp.einsum(
            "tgjn,ngd->tgjd",
            weights.astype(jnp.bfloat16),
            value_rows[first_key:last_key],
            preferred_element_type=jnp.float32,
        )
        running_max = new_max
    return (running_max, running_sum, weighted)


def body(
    queries,
    window_keys,
    window_values,
    anchor_keys,
    anchor_values,
    passing_rows,
    block_of_device,
    out_weight,
):
    tok_rows, head_count, head_size = queries.shape
    kv_local = window_keys.shape[1]
    group_size = head_count // kv_local
    retained = passing_rows.shape[1]
    grouped = queries.reshape(tok_rows, kv_local, group_size, head_size)
    my_slot = lax.axis_index(CTX)
    own_block = lookup(block_of_device, jnp.reshape(my_slot, (1,)))[0]
    fold_state = (
        jnp.full((tok_rows, kv_local, group_size), -1e30, jnp.float32),
        jnp.zeros((tok_rows, kv_local, group_size), jnp.float32),
        jnp.zeros((tok_rows, kv_local, group_size, head_size), jnp.float32),
    )
    places = jnp.arange(tok_rows, dtype=jnp.int32)
    causal = places[None, :] <= places[:, None]
    fold_state = attend(fold_state, grouped, window_keys, window_values, causal)
    shard_piece = side_by_side(
        (anchor_keys, anchor_values), (("ctx_0", "ctx_1", "ctx_2"), "ctx_3"), 0, 1
    )
    seen_all = jnp.ones((1, shard_piece[0].shape[0]), dtype=bool)
    fold_state = attend(fold_state, grouped, shard_piece[0], shard_piece[1], seen_all)
    chosen = lax.dynamic_slice_in_dim(passing_rows, my_slot, 1, 0)[0]
    picked_keys = jnp.take(window_keys, chosen, axis=0)
    picked_values = jnp.take(window_values, chosen, axis=0)
    shard_piece = side_by_side_2((picked_keys, picked_values), CTX, 0, 1)
    rows_here = shard_piece[0].shape[0]
    slot_ids = jnp.arange(rows_here, dtype=jnp.int32) // retained
    earlier = lookup(block_of_device, slot_ids) < own_block
    fold_state = attend(fold_state, grouped, shard_piece[0], shard_piece[1], earlier[None, :])
    running_max, running_sum, weighted = fold_state
    attended = (
        (weighted / running_sum[..., None])
        .reshape(tok_rows, head_count * head_size)
        .astype(jnp.bfloat16)
    )
    mixed = sent_and_summed(
        lax.dot_general(
            out_weight, attended, (((1,), (1,)), ((), ())), preferred_element_type=jnp.float32
        ).astype(jnp.bfloat16),
        "tp",
        0,
    )
    return mixed.astype(jnp.bfloat16)


def solution(mesh):
    torus = Mesh(
        mesh.devices.reshape(4, 2, 4, 2, mesh.shape["tp"]),
        ("ctx_0", "ctx_1", "ctx_2", "ctx_3", "tp"),
    )
    return jax.shard_map(
        body,
        mesh=torus,
        in_specs=(
            P(CTX, "tp", None),
            P(CTX, "tp", None),
            P(CTX, "tp", None),
            P(CTX, "tp", None),
            P(CTX, "tp", None),
            P(),
            P(),
            P(None, "tp"),
        ),
        out_specs=P("tp", CTX),
        check_vma=False,
    )
```

profile of v0, /device:TPU:1, one launch (start us, length us, event | category | flops | bytes accessed | tf_op | source)
XLA Modules:
  0.0 164.8 jit_solution(14609109782034434194)
XLA Ops:
  6.5 0.8 pad_maximum_fusion
  7.3 1.2 broadcast_in_dim.163
  8.6 14.5 %all-to-all-start = ((bf16[32,64,2,128]{3,1,2,0:T(8,128)(2,1)}), bf16[32,64,2,128]{3,1,2,0:T(8,128)(2,1)S(1)}, u32[]{:S(2)}, u32[]{:S(2)}) async-start(bf16[32,64,2,128]{3,1,2,0:T(8,128)(2,1)} %broadcast_in_dim.163), calls=%async_computation | async-start | bytes 2097152 | tf_op jit(solution)/shard_map/all_to_all | solution.py:12
  23.1 0.9 dynamic-slice_reduce_fusion
  24.0 1.3 gather_fusion.1
  25.4 1.3 gather_fusion
  27.4 1.4 fusion.120
  28.8 0.8 select_reduce_fusion
  30.4 1.0 fusion.135
  31.4 13.5 %all-to-all-done = bf16[32,64,2,128]{3,1,2,0:T(8,128)(2,1)S(1)} async-done(((bf16[32,64,2,128]{3,1,2,0:T(8,128)(2,1)}), bf16[32,64,2,128]{3,1,2,0:T(8,128)(2,1)S(1)}, u32[]{:S(2)}, u32[]{:S(2)}) %all-to-all-start) | async-done | bytes 1048608 | tf_op jit(solution)/shard_map/all_to_all | solution.py:12
  45.7 6.9 %all_to_all.15 = bf16[2,32,64,2,128]{4,2,1,3,0:T(8,128)(2,1)S(1)} all-to-all(bf16[2,32,64,2,128]{4,2,1,3,0:T(8,128)(2,1)S(1)} %broadcast_in_dim.164), channel_id=1, replica_groups=mesh['ctx_0'=4,'ctx_1'=2,'ctx_2'=4,'ctx_3'=2,'tp'=4] {'ctx_3'}, dimensions={0} | all-to-all | bytes 4194304 | tf_op jit(solution)/shard_map/all_to_all | solution.py:12
  52.8 2.6 %bitcast_reduce_fusion.2 = (f32[128,8]{0,1:T(8,128)S(1)}, f32[1024,128,8]{1,0,2:T(8,128)}) fusion(bf16[128,8,128]{2,1,0:T(8,128)(2,1)S(1)} %copy-done, bf16[4096,2,128]{2,0,1:T(8,128)(2,1)S(1)} %bitcast.339), kind=kOutput, calls=%fused_computation.14 | convolution fusion | flops 270531584 | bytes 4722688 | tf_op jit(solution)/shard_map/tgjd,ngd->tgjn/dot_general | solution.py:69
  55.4 2.7 %bitcast_reduce_fusion.3 = (f32[128,8]{0,1:T(8,128)S(1)}, f32[1024,128,8]{1,0,2:T(8,128)}) fusion(bf16[128,8,128]{2,1,0:T(8,128)(2,1)S(1)} %copy-done, bf16[4096,2,128]{2,0,1:T(8,128)(2,1)S(1)} %bitcast.340), kind=kOutput, calls=%fused_computation.17 | convolution fusion | flops 270531584 | bytes 4722688 | tf_op jit(solution)/shard_map/tgjd,ngd->tgjn/dot_general | solution.py:69
  58.1 2.7 %bitcast_reduce_fusion.4 = (f32[128,8]{0,1:T(8,128)S(1)}, f32[1024,128,8]{1,0,2:T(8,128)}) fusion(bf16[128,8,128]{2,1,0:T(8,128)(2,1)S(1)} %copy-done, bf16[4096,2,128]{2,0,1:T(8,128)(2,1)S(1)} %bitcast.341), kind=kOutput, calls=%fused_computation.20 | convolution fusion | flops 270531584 | bytes 4722688 | tf_op jit(solution)/shard_map/tgjd,ngd->tgjn/dot_general | solution.py:69
  60.8 2.7 %bitcast_reduce_fusion.5 = (f32[128,8]{0,1:T(8,128)S(1)}, f32[1024,128,8]{1,0,2:T(8,128)}) fusion(bf16[128,8,128]{2,1,0:T(8,128)(2,1)S(1)} %copy-done, bf16[4096,2,128]{2,0,1:T(8,128)(2,1)S(1)} %bitcast.342), kind=kOutput, calls=%fused_computation.23 | convolution fusion | flops 270531584 | bytes 4722688 | tf_op jit(solution)/shard_map/tgjd,ngd->tgjn/dot_general | solution.py:69
  63.5 43.9 %all-gather.2.cloned.1.call-done = bf16[2048,2,128]{2,0,1:T(8,128)(2,1)} async-done(((bf16[32,2,128]{2,0,1:T(8,128)(2,1)}), bf16[2048,2,128]{2,0,1:T(8,128)(2,1)}) %all-gather.2.cloned.1.call-update) | async-done | bytes 1048592 | tf_op jit(solution)/shard_map/all_gather | solution.py:40
  107.3 1.8 %bitcast_reduce_fusion = (f32[128,8]{0,1:T(8,128)S(1)}, f32[1024,128,8]{1,0,2:T(8,128)S(1)}) fusion(pred[1024]{0:T(1024)(128)(4,1)S(1)} %get-tuple-element.6, bf16[128,8,128]{2,1,0:T(8,128)(2,1)S(1)} %copy-done, bf16[2048,2,128]{2,0,1:T(8,128)(2,1)} %all-gather.2.cloned.1.call-done), kind=kOutput, calls=%fused_computation.4 | convolution fusion | flops 271580160 | bytes 4723712 | tf_op jit(solution)/shard_map/tgjd,ngd->tgjn/dot_general | solution.py:69
  109.2 0.7 bitcast_reduce_fusion.1
  110.0 0.9 fusion.65
  111.6 1.4 fusion.12
  113.0 0.9 fusion.62
  113.9 1.2 copy-done.1
  115.1 0.9 fusion.59
  116.4 1.4 fusion.8
  117.8 0.9 fusion.56
  118.9 2.8 %fusion.16 = (f32[128,8]{0,1:T(8,128)S(1)}, f32[128,8]{0,1:T(8,128)S(1)}) fusion(f32[1024,128,8]{1,0,2:T(8,128)S(1)} %get-tuple-element.28, f32[128,8]{0,1:T(8,128)S(1)} %get-tuple-element.16, pred[1024]{0:T(1024)(128)(4,1)S(1)} %get-tuple-element.7, f32[128,8]{0,1:T(8,128)S(1)} %get-tuple-element.15, f32[1024,128,8]{1,0,2:T(8,128)S(1)} %get-tuple-element.26, ...), kind=kLoop, calls=%fused_computation.33 | loop fusion | flops 10483712 | bytes 8407040 | tf_op jit(solution)/shard_map/reduce_sum | solution.py:81
  122.2 1.4 fusion.72
  123.6 1.4 fusion.92
  125.0 1.0 slice-done.1
  126.0 2.8 %convolution_convert_fusion = bf16[128,4096]{1,0:T(8,128)(2,1)S(1)} fusion(bf16[128,1024]{0,1:T(8,128)(2,1)S(1)} %bitcast.351, bf16[4096,1024]{1,0:T(8,128)(2,1)S(1)} %bitcast.337), kind=kOutput, calls=%fused_computation.2 | convolution fusion | flops 1074266112 | bytes 9699328 | tf_op jit(solution)/shard_map/dot_general | solution.py:137
  128.9 28.0 %all_to_all.16 = bf16[4,1024,128]{1,2,0:T(8,128)(2,1)S(1)} all-to-all(bf16[4,1024,128]{1,2,0:T(8,128)(2,1)S(1)} %bitcast.348), channel_id=1, replica_groups=mesh['ctx_0'=4,'ctx_1'=2,'ctx_2'=4,'ctx_3'=2,'tp'=4] {'tp'}, dimensions={0} | all-to-all | bytes 2097152 | tf_op jit(solution)/shard_map/all_to_all | solution.py:52
  157.1 0.8 copy.102
  (38 shorter events, 4.3 us)
Async XLA Ops:
  6.5 23.9 %copy-start = (bf16[128,8,128]{2,1,0:T(8,128)(2,1)S(1)}, bf16[128,8,128]{2,1,0:T(8,128)(2,1)}, u32[]{:S(2)}) copy-start(bf16[128,8,128]{2,1,0:T(8,128)(2,1)} %param.10) | copy-start | bytes 786436
  8.6 36.4 %all-to-all-start = ((bf16[32,64,2,128]{3,1,2,0:T(8,128)(2,1)}), bf16[32,64,2,128]{3,1,2,0:T(8,128)(2,1)S(1)}, u32[]{:S(2)}, u32[]{:S(2)}) async-start(bf16[32,64,2,128]{3,1,2,0:T(8,128)(2,1)} %broadcast_in_dim.163), calls=%async_computation | async-start | bytes 2097152 | tf_op jit(solution)/shard_map/all_to_all | solution.py:12
  23.1 84.3 %all-gather.2.cloned.1.call-start = ((), (), s32[]{:S(2)}) async-start(), calls=%async_computation.3 | async-start | bytes 1064960 | tf_op jit(solution)/shard_map/all_gather | solution.py:40
  107.3 1.9 %copy-start.6 = (bf16[2048,2,128]{2,0,1:T(8,128)(2,1)S(1)}, bf16[2048,2,128]{2,0,1:T(8,128)(2,1)}, u32[]{:S(2)}) copy-start(bf16[2048,2,128]{2,0,1:T(8,128)(2,1)} %all-gather.2.cloned.1.call-done) | copy-start | bytes 3145732
  107.3 2.7 %copy-start.3 = (f32[1024,128,8]{1,0,2:T(8,128)S(1)}, f32[1024,128,8]{1,0,2:T(8,128)}, u32[]{:S(2)}) copy-start(f32[1024,128,8]{1,0,2:T(8,128)} %get-tuple-element.30) | copy-start | bytes 12582916
  109.2 2.4 %copy-start.4 = (f32[1024,128,8]{1,0,2:T(8,128)S(1)}, f32[1024,128,8]{1,0,2:T(8,128)}, u32[]{:S(2)}) copy-start(f32[1024,128,8]{1,0,2:T(8,128)} %get-tuple-element.32) | copy-start | bytes 12582916
  112.9 2.2 %copy-start.1 = (f32[1024,128,8]{1,0,2:T(8,128)S(1)}, f32[1024,128,8]{1,0,2:T(8,128)}, u32[]{:S(2)}) copy-start(f32[1024,128,8]{1,0,2:T(8,128)} %get-tuple-element.34) | copy-start | bytes 12582916
  113.0 3.5 %copy-start.2 = (f32[1024,128,8]{1,0,2:T(8,128)S(1)}, f32[1024,128,8]{1,0,2:T(8,128)}, u32[]{:S(2)}) copy-start(f32[1024,128,8]{1,0,2:T(8,128)} %get-tuple-element.36) | copy-start | bytes 12582916
  118.9 2.9 %copy-start.5 = (bf16[128,1,128]{2,0,1:T(8,128)(2,1)S(1)}, bf16[128,1,128]{2,0,1:T(8,128)(2,1)}, u32[]{:S(2)}) copy-start(bf16[128,1,128]{2,0,1:T(8,128)(2,1)} %param.12) | copy-start | bytes 98308
  122.2 2.8 %slice-start = ((s8[8388608]{0:T(1024)(128)(4,1)}), s8[4194304]{0:T(1024)(128)(4,1)S(1)}, s32[]{:S(2)}) async-start(s8[8388608]{0:T(1024)(128)(4,1)} %bitcast.336), calls=%async_computation.4 | async-start | bytes 8388608
  123.6 2.4 %slice-start.1 = ((s8[8388608]{0:T(1024)(128)(4,1)}), s8[4194304]{0:T(1024)(128)(4,1)S(1)}, s32[]{:S(2)}) async-start(s8[8388608]{0:T(1024)(128)(4,1)} %bitcast.336), calls=%async_computation.5 | async-start | bytes 8388608
Sparse Core Ops, SparseCore 0:
  27.6 79.7 all-gather.1
where the time goes:
time: 165 us
  waiting for transfers between devices  57.4 us (35%)
  blocking collectives  34.9 us (21%)
  matrix products  24 us (15%)
  starting transfers between devices  14.5 us (9%)
  between operations  13.7 us (8%)
  other arithmetic  10.4 us (6%)
  local copies, waits for them, and re-layouts  9.93 us (6%)
    all_gather x1, waiting for transfers between devices, side_by_side_2(): filled = lax.all_gather(both, axis, axis=dim, tiled=True)  43.9 us
    all_to_all x1, blocking collectives, sent_and_summed(): lax.all_to_all(parts, axis, split_axis=0, concat_axis=0, tiled=True)  28 us
    all_to_all x1, starting transfers between devices, copy_for_each(): lax.all_to_all(jnp.broadcast_to(array[None], (size, *array.shape)), axis,...  14.5 us
    dot_general x7, matrix products, attend(): jnp.einsum('tgjd,ngd->tgjn', grouped, key_rows[first_key:last_key], prefe...  14.3 us
    all_to_all x1, waiting for transfers between devices, copy_for_each(): lax.all_to_all(jnp.broadcast_to(array[None], (size, *array.shape)), axis,...  13.5 us
    all_to_all x1, blocking collectives, copy_for_each(): lax.all_to_all(jnp.broadcast_to(array[None], (size, *array.shape)), axis,...  6.93 us
    dot_general x7, matrix products, attend(): jnp.einsum('tgjn,ngd->tgjd', weights.astype(jnp.bfloat16), value_rows[fir...  6.86 us
    reduce_sum x4, other arithmetic, attend(): running_sum = running_sum * factor + jnp.sum(weights, axis=-1)  5.72 us
  transfers between devices with their start and end apart: 2, of which 2 were waited for; matrix products, arithmetic and copies ran while one was open for 12% of the time, Pallas kernels for 0%

commit v1 on v0

v1 whole, which is shorter than its diff:
```python
import math

import jax
import jax.numpy as jnp
from jax import lax
from jax.experimental import pallas as pl
from jax.experimental.pallas import tpu as pltpu
from jax.sharding import PartitionSpec as P

MESH = pl.DeviceIdType.MESH
RING = 4
HALVES = 2
F32 = jnp.float32
BF16 = jnp.bfloat16
NEG = -1e30
QB = 256
CHUNKS = 4


def kernel(
    wk_ref,
    wv_ref,
    ak_ref,
    av_ref,
    prt_ref,
    bod_ref,
    q_hbm,
    w_hbm,
    out_ref,
    g,
    q32,
    qh,
    w,
    m_ref,
    acc,
    vt,
    at,
    own,
    part,
    sbuf,
    rbuf,
    load_sem,
    gs_sem,
    gr_sem,
    ps_sem,
    pr_sem,
    ts_sem,
    tr_sem,
    tok,
    heads,
):
    anch = ak_ref.shape[0]
    ret = prt_ref.shape[0]
    keys = anch + ret
    hd = ak_ref.shape[1]
    half = keys
    ctx = lax.axis_index("ctx")
    tp = lax.axis_index("tp")
    core = lax.rem(ctx, 2)
    y = lax.rem(ctx // 2, RING)
    zh = lax.rem(ctx // (2 * RING), 2)
    x = ctx // (4 * RING)

    def slot_of(xx, zz, yy, cc):
        return ((xx * 2 + zz) * RING + yy) * 2 + cc

    def step_along(first, by):
        dx = core + first - 2 * core * first
        xx = lax.rem(x + (1 - dx) * by + RING, RING)
        yy = lax.rem(y + dx * by + RING, RING)
        return slot_of(xx, zh, yy, core)

    dev = {
        "f+": (step_along(0, 1), tp),
        "f-": (step_along(0, -1), tp),
        "s+": (step_along(1, 1), tp),
        "s-": (step_along(1, -1), tp),
        "z": (slot_of(x, 1 - zh, y, core), tp),
        "c": (slot_of(x, zh, y, 1 - core), tp),
    }

    q_load = pltpu.make_async_copy(q_hbm, q32, load_sem.at[0])
    w_load = pltpu.make_async_copy(w_hbm, w, load_sem.at[1])
    q_load.start()
    w_load.start()

    barrier = pltpu.get_barrier_semaphore()
    for d in dev.values():
        pl.semaphore_signal(barrier, inc=1, device_id=d, device_id_type=MESH)
    for k in range(1, 4):
        pl.semaphore_signal(
            barrier, inc=1, device_id=(ctx, lax.rem(tp + k, 4)), device_id_type=MESH
        )

    lane = lax.broadcasted_iota(jnp.int32, prt_ref.shape, 1)
    mine = jnp.where(lane == ctx, prt_ref[...], 0).astype(F32)
    chosen = jnp.sum(mine, axis=1, keepdims=True).astype(jnp.int32)
    pick = (lax.broadcasted_iota(jnp.int32, (ret, tok), 1) == chosen).astype(F32).astype(BF16)
    g[0, 0, 0, 0, 0:anch, :] = ak_ref[...]
    g[0, 0, 0, 0, keys : keys + anch, :] = av_ref[...]
    g[0, 0, 0, 0, anch:keys, :] = jnp.dot(
        pick, wk_ref[...], preferred_element_type=F32
    ).astype(BF16)
    g[0, 0, 0, 0, keys + anch : 2 * keys, :] = jnp.dot(
        pick, wv_ref[...], preferred_element_type=F32
    ).astype(BF16)

    pending = []
    count = [0]

    def remote(src, dst, recv, to):
        copy = pltpu.make_async_remote_copy(
            src_ref=src,
            dst_ref=dst,
            send_sem=gs_sem.at[count[0]],
            recv_sem=recv,
            device_id=dev[to],
            device_id_type=MESH,
        )
        count[0] += 1
        copy.start()
        pending.append(copy)

    def sem(z, d2, d1):
        return gr_sem.at[(z * RING + d2) * RING + d1]

    def arrived(z, d2, d1):
        ref = g.at[z, d2, 0, d1]
        if d2 == 0 and d1 == 2:
            for h in range(2):
                r = ref.at[pl.ds(h * half, half)]
                s = gr_sem.at[32 + z * 2 + h]
                pltpu.make_async_copy(r, r, s).wait()
        else:
            pltpu.make_async_copy(ref, ref, sem(z, d2, d1)).wait()

    def to_partner(z, d2, d1):
        remote(
            g.at[z, d2, 0, d1],
            g.at[z, d2, 1, d1],
            pr_sem.at[(z * RING + d2) * RING + d1],
            "c",
        )

    def second_both(z, d1):
        remote(g.at[z, 0, 0, d1], g.at[z, 3, 0, d1], sem(z, 3, d1), "s+")
        remote(g.at[z, 0, 0, d1], g.at[z, 1, 0, d1], sem(z, 1, d1), "s-")

    def start_own(z):
        remote(g.at[z, 0, 0, 0], g.at[z, 0, 0, 3], sem(z, 0, 3), "f+")
        remote(g.at[z, 0, 0, 0], g.at[z, 0, 0, 1], sem(z, 0, 1), "f-")
        second_both(z, 0)

    def after_first(z):
        for d1, to, h in ((3, "f+", 0), (1, "f-", 1)):
            arrived(z, 0, d1)
            rows = pl.ds(h * half, half)
            remote(
                g.at[z, 0, 0, d1, rows],
                g.at[z, 0, 0, 2, rows],
                gr_sem.at[32 + z * 2 + h],
                to,
            )
            second_both(z, d1)
            to_partner(z, 0, d1)

    def after_first_2(z):
        arrived(z, 0, 2)
        second_both(z, 2)
        to_partner(z, 0, 2)

    def after_second(z, d1):
        for d2, to in ((3, "s+"), (1, "s-")):
            arrived(z, d2, d1)
            if (d2 == 3) == (d1 in (0, 1)):
                remote(g.at[z, d2, 0, d1], g.at[z, 2, 0, d1], sem(z, 2, d1), to)
            to_partner(z, d2, d1)

    def after_second_2(z):
        for d1 in range(RING):
            arrived(z, 2, d1)
            to_partner(z, 2, d1)

    scale = (hd**-0.5) * math.log2(math.e)
    own_block = bod_ref[ctx]

    def fold(s, cols, n, first):
        top = jnp.max(s, axis=0, keepdims=True)
        if first:
            new = top
        else:
            old = m_ref[0:1, cols]
            new = jnp.maximum(old, top)
        p = jnp.exp2((s - new) * scale).astype(BF16)
        add = jnp.dot(vt[:, 0:n], p, preferred_element_type=F32)
        if first:
            acc[:, cols] = add
        else:
            acc[:, cols] = acc[:, cols] * jnp.exp2((old - new) * scale) + add
        m_ref[0:1, cols] = new

    def local_pass():
        vt[0:hd, 0:tok] = wv_ref[...].T
        row = lax.broadcasted_iota(jnp.int32, (tok, QB), 0)
        col = lax.broadcasted_iota(jnp.int32, (tok, QB), 1)
        seen = row <= lax.rem(col, tok)

        def block(i, c):
            cols = pl.ds(pl.multiple_of(i * QB, QB), QB)
            s = lax.dot_general(
                wk_ref[...], qh[cols, :], (((1,), (1,)), ((), ())), preferred_element_type=F32
            )
            fold(jnp.where(seen, s, NEG), cols, tok, True)
            return c

        lax.fori_loop(0, tok * heads // QB, block, 0)

    def compute(z, d2):
        for d1 in range(RING):
            r = g.at[z, d2, 1, d1]
            pltpu.make_async_copy(r, r, pr_sem.at[(z * RING + d2) * RING + d1]).wait()
        n = 2 * RING * keys
        vt[0:hd, 0:n] = g[z, d2, :, :, keys : 2 * keys, :].reshape(n, hd).T
        bias = []
        zz = zh if z == 0 else 1 - zh
        for s in range(2):
            cc = core if s == 0 else 1 - core
            for d1 in range(RING):
                dx = lax.rem(x + (1 - cc) * d1 + cc * d2, RING)
                dy = lax.rem(y + cc * d1 + (1 - cc) * d2, RING)
                bias.append(
                    jnp.where(bod_ref[slot_of(dx, zz, dy, cc)] < own_block, 0.0, NEG).astype(F32)
                )

        def block(i, c):
            cols = pl.ds(pl.multiple_of(i * QB, QB), QB)
            k = g[z, d2, :, :, 0:keys, :].reshape(n, hd)
            s = lax.dot_general(
                k, qh[cols, :], (((1,), (1,)), ((), ())), preferred_element_type=F32
            )
            parts = []
            for j in range(2 * RING):
                parts.append(s[j * keys : j * keys + anch])
                parts.append(s[j * keys + anch : (j + 1) * keys] + bias[j])
            fold(jnp.concatenate(parts, axis=0), cols, n, False)
            return c

        lax.fori_loop(0, tok * heads // QB, block, 0)

    pl.semaphore_wait(barrier, 9)
    start_own(0)
    remote(g.at[0, 0, 0, 0], g.at[1, 0, 0, 0], sem(1, 0, 0), "z")
    to_partner(0, 0, 0)

    q_load.wait()
    qh32 = q32[...].astype(F32)
    own[...] = qh32
    for h in range(heads):
        qh[h * tok : (h + 1) * tok, :] = own[pl.ds(h, tok, stride=heads), :].astype(BF16)
    vt[hd:, :] = jnp.ones((vt.shape[0] - hd, vt.shape[1]), BF16)
    local_pass()

    after_first(0)
    after_second(0, 0)
    after_first_2(0)
    after_second(0, 3)
    after_second(0, 1)
    compute(0, 0)
    arrived(1, 0, 0)
    start_own(1)
    to_partner(1, 0, 0)
    after_second(0, 2)
    after_first(1)
    after_second_2(0)
    compute(0, 1)
    after_second(1, 0)
    after_first_2(1)
    compute(0, 3)
    after_second(1, 3)
    after_second(1, 1)
    compute(0, 2)
    compute(1, 0)
    after_second(1, 2)
    compute(1, 1)
    after_second_2(1)
    compute(1, 3)
    compute(1, 2)

    for h in range(heads):
        cols = slice(h * tok, (h + 1) * tok)
        at[h * hd : (h + 1) * hd, :] = (
            acc[0:hd, cols] * (1.0 / acc[hd : hd + 1, cols])
        ).astype(BF16)

    side = tp // 2
    u = (1 - side) * tp + side * (3 - tp)

    def real(e):
        return (1 - side) * e + side * (3 - e)

    def pick2(edge, inner):
        return (1 - u) * edge + u * inner

    feats = out_ref.shape[0]
    rows = feats // CHUNKS
    w_load.wait()

    def product(e, ck):
        at_row = pl.multiple_of(e * feats + ck * rows, rows)
        return jnp.dot(w[pl.ds(at_row, rows), :], at[...], preferred_element_type=F32)

    def tp_copy(ph, ck, to, slot):
        r = pl.ds(pl.multiple_of(ck * rows, rows), rows)
        return pltpu.make_async_remote_copy(
            src_ref=sbuf.at[ph, r],
            dst_ref=rbuf.at[slot, r],
            send_sem=ts_sem.at[ph * CHUNKS + ck],
            recv_sem=tr_sem.at[slot * CHUNKS + ck],
            device_id=(ctx, to),
            device_id_type=MESH,
        )

    def landed(slot, ck):
        r = rbuf.at[slot, pl.ds(pl.multiple_of(ck * rows, rows), rows)]
        pltpu.make_async_copy(r, r, tr_sem.at[slot * CHUNKS + ck]).wait()

    plan = (
        (real(pick2(3, 2)), real(pick2(1, 2)), pick2(3, 1)),
        (real(pick2(2, 0)), real(pick2(2, 0)), pick2(2, 0)),
        (real(pick2(1, 3)), real(pick2(1, 3)), pick2(0, 1)),
    )

    def send_block(ph):
        e, to, slot = plan[ph]

        def one(ck, c):
            r = pl.ds(pl.multiple_of(ck * rows, rows), rows)
            if ph < 2:
                sbuf[ph, r, :] = product(e, ck).astype(BF16)
            else:
                part[...] = product(e, ck)

                @pl.when(u == 1)
                def _():
                    landed(3, ck)
                    part[...] += rbuf[3, r, :].astype(F32)

                sbuf[ph, r, :] = part[...].astype(BF16)
            tp_copy(ph, ck, to, slot).start()
            return c

        lax.fori_loop(0, CHUNKS, one, 0)

    send_block(0)
    send_block(1)

    def own_part(ck, c):
        r = pl.ds(pl.multiple_of(ck * rows, rows), rows)
        own[r, :] = product(tp, ck)
        return c

    lax.fori_loop(0, CHUNKS, own_part, 0)
    send_block(2)

    def finish(ck, c):
        r = pl.ds(pl.multiple_of(ck * rows, rows), rows)

        @pl.when(u == 1)
        def _():
            landed(2, ck)
            own[r, :] += rbuf[2, r, :].astype(F32)

        landed(0, ck)
        landed(1, ck)
        out_ref[r, :] = (
            own[r, :] + rbuf[0, r, :].astype(F32) + rbuf[1, r, :].astype(F32)
        ).astype(BF16)
        return c

    lax.fori_loop(0, CHUNKS, finish, 0)

    for copy in pending:
        copy.wait_send()
    for ph in range(3):
        e, to, slot = plan[ph]

        def drain(ck, c, ph=ph, to=to, slot=slot):
            tp_copy(ph, ck, to, slot).wait_send()
            return c

        lax.fori_loop(0, CHUNKS, drain, 0)


def body(
    queries,
    window_keys,
    window_values,
    anchor_keys,
    anchor_values,
    passing_rows,
    block_of_device,
    out_weight,
):
    tok, heads, hd = queries.shape
    anch = anchor_keys.shape[0]
    ret = passing_rows.shape[1]
    dout = out_weight.shape[0]
    feats = dout // lax.axis_size("tp")
    keys = anch + ret
    n = 2 * RING * keys
    vm = pl.BlockSpec(memory_space=pltpu.VMEM)
    sends = 2 * (4 + 12 + 16) + 1

    def run(*refs):
        kernel(*refs, tok=tok, heads=heads)

    return pl.pallas_call(
        run,
        out_shape=jax.ShapeDtypeStruct((feats, tok), BF16),
        in_specs=[vm] * 5
        + [
            pl.BlockSpec(memory_space=pltpu.SMEM),
            pl.BlockSpec(memory_space=pl.ANY),
            pl.BlockSpec(memory_space=pl.ANY),
        ],
        out_specs=vm,
        scratch_shapes=[
            pltpu.VMEM((HALVES, RING, 2, RING, 2 * keys, hd), BF16),
            pltpu.VMEM((tok * heads, hd), BF16),
            pltpu.VMEM((tok * heads, hd), BF16),
            pltpu.VMEM(out_weight.shape, BF16),
            pltpu.VMEM((8, tok * heads), F32),
            pltpu.VMEM((hd + 16, tok * heads), F32),
            pltpu.VMEM((hd + 16, n), BF16),
            pltpu.VMEM((heads * hd, tok), BF16),
            pltpu.VMEM((feats, tok), F32),
            pltpu.VMEM((feats // CHUNKS, tok), F32),
            pltpu.VMEM((3, feats, tok), BF16),
            pltpu.VMEM((4, feats, tok), BF16),
            pltpu.SemaphoreType.DMA((2,)),
            pltpu.SemaphoreType.DMA((sends,)),
            pltpu.SemaphoreType.DMA((36,)),
            pltpu.SemaphoreType.DMA((1,)),
            pltpu.SemaphoreType.DMA((32,)),
            pltpu.SemaphoreType.DMA((3 * CHUNKS,)),
            pltpu.SemaphoreType.DMA((4 * CHUNKS,)),
        ],
        compiler_params=pltpu.CompilerParams(collective_id=0, has_side_effects=True),
        name="layer",
    )(
        window_keys.reshape(tok, hd),
        window_values.reshape(tok, hd),
        anchor_keys.reshape(anch, hd),
        anchor_values.reshape(anch, hd),
        passing_rows.T,
        block_of_device,
        queries.reshape(tok * heads, hd),
        out_weight,
    )


def solution(mesh):
    return jax.shard_map(
        body,
        mesh=mesh,
        in_specs=(
            P("ctx", "tp", None),
            P("ctx", "tp", None),
            P("ctx", "tp", None),
            P("ctx", "tp", None),
            P("ctx", "tp", None),
            P(),
            P(),
            P(None, "tp"),
        ),
        out_specs=P("tp", "ctx"),
        check_vma=False,
    )
```

time: 165 us -> 69 us (0.42)
  Pallas kernels: 0 us -> 67.1 us
  waiting for transfers between devices: 57.4 us -> 0 us
  blocking collectives: 34.9 us -> 0 us
  matrix products: 24 us -> 0 us
  starting transfers between devices: 14.5 us -> 0 us
  between operations: 13.7 us -> 0.01 us
  other arithmetic: 10.4 us -> 0 us
  local copies, waits for them, and re-layouts: 9.93 us -> 1.67 us
    pallas_call x0 -> x1, Pallas kernels: none -> 67.1 us  [body(): pl.pallas_call(run, out_shape=jax.ShapeDtypeStruct((feats, tok), BF16), i...]
    all_gather x1 -> x0, waiting for transfers between devices: 43.9 us -> none  [side_by_side_2(): filled = lax.all_gather(both, axis, axis=dim, tiled=True)]
    all_to_all x2 -> x0, blocking collectives: 34.9 us -> none  [the longest x1 28 us: sent_and_summed(): lax.all_to_all(parts, axis, split_axis=0, concat_axis=0, tiled=True)]
    dot_general x15 -> x0, matrix products: 24 us -> none  [the longest x7 14.3 us: attend(): jnp.einsum('tgjd,ngd->tgjn', grouped, key_rows[first_key:last_key], prefe...]
    all_to_all x1 -> x0, starting transfers between devices: 14.5 us -> none  [copy_for_each(): lax.all_to_all(jnp.broadcast_to(array[None], (size, *array.shape)), axis,...]
    all_to_all x1 -> x0, waiting for transfers between devices: 13.5 us -> none  [copy_for_each(): lax.all_to_all(jnp.broadcast_to(array[None], (size, *array.shape)), axis,...]
    reduce_sum x7 -> x0, other arithmetic: 8.11 us -> none  [the longest x4 5.72 us: attend(): running_sum = running_sum * factor + jnp.sum(weights, axis=-1)]
    gather x2 -> x0, local copies, waits for them, and re-layouts: 2.68 us -> none  [the longest x1 1.34 us: body(): picked_values = jnp.take(window_values, chosen, axis=0)]
  transfers between devices with their start and end apart: 2 -> 0, of which waited for: 2 -> 0; matrix products, arithmetic and copies ran while one was open for 12% -> 0% of each run, Pallas kernels for 0% -> 0%
where the time goes in v1:
time: 69 us; the launch traced here: 68.8 us
  Pallas kernels  67.1 us (97%)
  local copies, waits for them, and re-layouts  1.67 us (2%)
    pallas_call x1, Pallas kernels, body(): pl.pallas_call(run, out_shape=jax.ShapeDtypeStruct((feats, tok), BF16), i...  67.1 us
    unnamed x1, local copies, waits for them, and re-layouts  1.67 us

profile of v1, /device:TPU:1, one launch (start us, length us, event | category | flops | bytes accessed | tf_op | source)
XLA Modules:
  0.0 68.8 jit_solution(5811493932493301041)
XLA Ops:
  0.0 67.1 %layer.1 = bf16[1024,128]{1,0:T(8,128)(2,1)} custom-call(bf16[128,128]{1,0:T(8,128)(2,1)} %bitcast.7, bf16[128,128]{1,0:T(8,128)(2,1)} %bitcast.8, bf16[64,128]{1,0:T(8,128)(2,1)} %bitcast.9, bf16[64,128]{1,0:T(8,128)(2,1)} %bitcast.10, s32[32,64]{1,0:T(8,128)} %bitcast.11, s32[64]{0:T(128)} %refs_5_.1, bf16[1024,128]{1,0:T(8,128)(2,1)} %bitcast.6, ...), custom_call_target="tpu_custom_call" | custom-call | tf_op jit(solution)/shard_map/layer/pallas_call | solution.py:417
  67.1 1.7 %copy.10 = bf16[1024,128]{1,0:T(8,128)(2,1)} copy(bf16[1024,128]{1,0:T(8,128)(2,1)} %layer.1) | data formatting | bytes 524288

commit v2 on v1

--- a/solution.py
+++ b/solution.py
@@ -18,15 +18,19 @@
 
 
 def kernel(
-    wk_ref,
-    wv_ref,
-    ak_ref,
-    av_ref,
-    prt_ref,
-    bod_ref,
+    wk_hbm,
+    wv_hbm,
+    ak_hbm,
+    av_hbm,
+    prt_hbm,
+    bod_hbm,
     q_hbm,
     w_hbm,
     out_ref,
+    wk_ref,
+    wv_ref,
+    prt_ref,
+    bod_ref,
     g,
     q32,
     qh,
@@ -42,17 +46,16 @@
     load_sem,
     gs_sem,
     gr_sem,
-    ps_sem,
     pr_sem,
     ts_sem,
     tr_sem,
     tok,
     heads,
 ):
-    anch = ak_ref.shape[0]
+    anch = ak_hbm.shape[0]
     ret = prt_ref.shape[0]
     keys = anch + ret
-    hd = ak_ref.shape[1]
+    hd = ak_hbm.shape[1]
     half = keys
     ctx = lax.axis_index("ctx")
     tp = lax.axis_index("tp")
@@ -79,11 +82,6 @@
         "c": (slot_of(x, zh, y, 1 - core), tp),
     }
 
-    q_load = pltpu.make_async_copy(q_hbm, q32, load_sem.at[0])
-    w_load = pltpu.make_async_copy(w_hbm, w, load_sem.at[1])
-    q_load.start()
-    w_load.start()
-
     barrier = pltpu.get_barrier_semaphore()
     for d in dev.values():
         pl.semaphore_signal(barrier, inc=1, device_id=d, device_id_type=MESH)
@@ -92,12 +90,27 @@
             barrier, inc=1, device_id=(ctx, lax.rem(tp + k, 4)), device_id_type=MESH
         )
 
+    def load(k, src, dst):
+        copy = pltpu.make_async_copy(src, dst, load_sem.at[k])
+        copy.start()
+        return copy
+
+    prt_load = load(0, prt_hbm, prt_ref)
+    wk_load = load(1, wk_hbm, wk_ref)
+    wv_load = load(2, wv_hbm, wv_ref)
+    ak_load = load(3, ak_hbm, g.at[0, 0, 0, 0, pl.ds(0, anch)])
+    av_load = load(4, av_hbm, g.at[0, 0, 0, 0, pl.ds(keys, anch)])
+    bod_load = load(5, bod_hbm, bod_ref)
+    q_load = load(6, q_hbm, q32)
+    w_load = load(7, w_hbm, w)
+
+    prt_load.wait()
     lane = lax.broadcasted_iota(jnp.int32, prt_ref.shape, 1)
     mine = jnp.where(lane == ctx, prt_ref[...], 0).astype(F32)
     chosen = jnp.sum(mine, axis=1, keepdims=True).astype(jnp.int32)
     pick = (lax.broadcasted_iota(jnp.int32, (ret, tok), 1) == chosen).astype(F32).astype(BF16)
-    g[0, 0, 0, 0, 0:anch, :] = ak_ref[...]
-    g[0, 0, 0, 0, keys : keys + anch, :] = av_ref[...]
+    wk_load.wait()
+    wv_load.wait()
     g[0, 0, 0, 0, anch:keys, :] = jnp.dot(
         pick, wk_ref[...], preferred_element_type=F32
     ).astype(BF16)
@@ -182,6 +195,9 @@
             to_partner(z, 2, d1)
 
     scale = (hd**-0.5) * math.log2(math.e)
+    ak_load.wait()
+    av_load.wait()
+    bod_load.wait()
     own_block = bod_ref[ctx]
 
     def fold(s, cols, n, first):
@@ -205,15 +221,21 @@
         col = lax.broadcasted_iota(jnp.int32, (tok, QB), 1)
         seen = row <= lax.rem(col, tok)
 
-        def block(i, c):
-            cols = pl.ds(pl.multiple_of(i * QB, QB), QB)
+        def scores(i):
             s = lax.dot_general(
-                wk_ref[...], qh[cols, :], (((1,), (1,)), ((), ())), preferred_element_type=F32
+                wk_ref[...],
+                qh[i * QB : (i + 1) * QB, :],
+                (((1,), (1,)), ((), ())),
+                preferred_element_type=F32,
             )
-            fold(jnp.where(seen, s, NEG), cols, tok, True)
-            return c
-
-        lax.fori_loop(0, tok * heads // QB, block, 0)
+            return jnp.where(seen, s, NEG)
+
+        blocks = tok * heads // QB
+        s = scores(0)
+        for i in range(blocks):
+            later = scores(i + 1) if i + 1 < blocks else None
+            fold(s, slice(i * QB, (i + 1) * QB), tok, True)
+            s = later
 
     def compute(z, d2):
         for d1 in range(RING):
@@ -232,20 +254,23 @@
                     jnp.where(bod_ref[slot_of(dx, zz, dy, cc)] < own_block, 0.0, NEG).astype(F32)
                 )
 
-        def block(i, c):
-            cols = pl.ds(pl.multiple_of(i * QB, QB), QB)
+        def scores(i):
             k = g[z, d2, :, :, 0:keys, :].reshape(n, hd)
             s = lax.dot_general(
-                k, qh[cols, :], (((1,), (1,)), ((), ())), preferred_element_type=F32
+                k, qh[i * QB : (i + 1) * QB, :], (((1,), (1,)), ((), ())), preferred_element_type=F32
             )
             parts = []
             for j in range(2 * RING):
                 parts.append(s[j * keys : j * keys + anch])
                 parts.append(s[j * keys + anch : (j + 1) * keys] + bias[j])
-            fold(jnp.concatenate(parts, axis=0), cols, n, False)
-            return c
-
-        lax.fori_loop(0, tok * heads // QB, block, 0)
+            return jnp.concatenate(parts, axis=0)
+
+        blocks = tok * heads // QB
+        s = scores(0)
+        for i in range(blocks):
+            later = scores(i + 1) if i + 1 < blocks else None
+            fold(s, slice(i * QB, (i + 1) * QB), n, False)
+            s = later
 
     pl.semaphore_wait(barrier, 9)
     start_own(0)
@@ -408,7 +433,6 @@
     feats = dout // lax.axis_size("tp")
     keys = anch + ret
     n = 2 * RING * keys
-    vm = pl.BlockSpec(memory_space=pltpu.VMEM)
     sends = 2 * (4 + 12 + 16) + 1
 
     def run(*refs):
@@ -417,14 +441,13 @@
     return pl.pallas_call(
         run,
         out_shape=jax.ShapeDtypeStruct((feats, tok), BF16),
-        in_specs=[vm] * 5
-        + [
-            pl.BlockSpec(memory_space=pltpu.SMEM),
-            pl.BlockSpec(memory_space=pl.ANY),
-            pl.BlockSpec(memory_space=pl.ANY),
-        ],
-        out_specs=vm,
+        in_specs=[pl.BlockSpec(memory_space=pltpu.HBM)] * 8,
+        out_specs=pl.BlockSpec(memory_space=pltpu.VMEM),
         scratch_shapes=[
+            pltpu.VMEM((tok, hd), BF16),
+            pltpu.VMEM((tok, hd), BF16),
+            pltpu.VMEM((ret, passing_rows.shape[0]), jnp.int32),
+            pltpu.SMEM(block_of_device.shape, jnp.int32),
             pltpu.VMEM((HALVES, RING, 2, RING, 2 * keys, hd), BF16),
             pltpu.VMEM((tok * heads, hd), BF16),
             pltpu.VMEM((tok * heads, hd), BF16),
@@ -437,25 +460,31 @@
             pltpu.VMEM((feats // CHUNKS, tok), F32),
             pltpu.VMEM((3, feats, tok), BF16),
             pltpu.VMEM((4, feats, tok), BF16),
-            pltpu.SemaphoreType.DMA((2,)),
+            pltpu.SemaphoreType.DMA((8,)),
             pltpu.SemaphoreType.DMA((sends,)),
             pltpu.SemaphoreType.DMA((36,)),
-            pltpu.SemaphoreType.DMA((1,)),
             pltpu.SemaphoreType.DMA((32,)),
             pltpu.SemaphoreType.DMA((3 * CHUNKS,)),
             pltpu.SemaphoreType.DMA((4 * CHUNKS,)),
         ],
-        compiler_params=pltpu.CompilerParams(collective_id=0, has_side_effects=True),
+        compiler_params=pltpu.CompilerParams(
+            collective_id=0, has_side_effects=True, vmem_limit_bytes=56_000_000
+        ),
         name="layer",
     )(
-        window_keys.reshape(tok, hd),
-        window_values.reshape(tok, hd),
-        anchor_keys.reshape(anch, hd),
-        anchor_values.reshape(anch, hd),
-        passing_rows.T,
-        block_of_device,
-        queries.reshape(tok * heads, hd),
-        out_weight,
+        *[
+            pltpu.with_memory_space_constraint(a, pltpu.HBM)
+            for a in (
+                window_keys.reshape(tok, hd),
+                window_values.reshape(tok, hd),
+                anchor_keys.reshape(anch, hd),
+                anchor_values.reshape(anch, hd),
+                passing_rows.T,
+                block_of_device,
+                queries.reshape(tok * heads, hd),
+                out_weight,
+            )
+        ]
     )
 
 

time: 69 us -> 58.4 us (0.85)
  Pallas kernels: 67.1 us -> 57.5 us
  local copies, waits for them, and re-layouts: 1.67 us -> 0.71 us
    pallas_call x1, Pallas kernels: 67.1 us -> 57.5 us  [body(): pl.pallas_call(run, out_shape=jax.ShapeDtypeStruct((feats, tok), BF16), i...]
    unnamed x1, local copies, waits for them, and re-layouts: 1.67 us -> 0.71 us
where the time goes in v2:
time: 58.4 us; the launch traced here: 58.2 us
  Pallas kernels  57.5 us (98%)
  local copies, waits for them, and re-layouts  0.71 us (1%)
    pallas_call x1, Pallas kernels, body(): pl.pallas_call(run, out_shape=jax.ShapeDtypeStruct((feats, tok), BF16), i...  57.5 us

profile of v2, /device:TPU:1, one launch (start us, length us, event | category | flops | bytes accessed | tf_op | source)
XLA Modules:
  0.0 58.2 jit_solution(3663940855283417911)
XLA Ops:
  0.0 57.5 %layer.1 = bf16[1024,128]{1,0:T(8,128)(2,1)S(1)} custom-call(bf16[128,128]{1,0:T(8,128)(2,1)} %bitcast.7, bf16[128,128]{1,0:T(8,128)(2,1)} %bitcast.8, bf16[64,128]{1,0:T(8,128)(2,1)} %bitcast.9, bf16[64,128]{1,0:T(8,128)(2,1)} %bitcast.10, s32[32,64]{1,0:T(8,128)} %bitcast.11, s32[64]{0:T(128)} %refs_5_.1, bf16[1024,128]{1,0:T(8,128)(2,1)} %bitcast.6, ...), custom_call_target="tpu_custom_call" | custom-call | tf_op jit(solution)/shard_map/layer/pallas_call | solution.py:441
  57.5 0.7 %copy.10 = bf16[1024,128]{1,0:T(8,128)(2,1)} copy(bf16[1024,128]{1,0:T(8,128)(2,1)S(1)} %layer.1) | data formatting | bytes 524288

commit v3 on v2

--- a/solution.py
+++ b/solution.py
@@ -13,8 +13,9 @@
 F32 = jnp.float32
 BF16 = jnp.bfloat16
 NEG = -1e30
-QB = 256
+QB = 512
 CHUNKS = 4
+DIRECT = ((2,), (2,))
 
 
 def kernel(
@@ -56,7 +57,6 @@
     ret = prt_ref.shape[0]
     keys = anch + ret
     hd = ak_hbm.shape[1]
-    half = keys
     ctx = lax.axis_index("ctx")
     tp = lax.axis_index("tp")
     core = lax.rem(ctx, 2)
@@ -64,6 +64,9 @@
     zh = lax.rem(ctx // (2 * RING), 2)
     x = ctx // (4 * RING)
 
+    def spot(z, d2, s, d1):
+        return ((z * RING + d2) * 2 + s) * RING + d1
+
     def slot_of(xx, zz, yy, cc):
         return ((xx * 2 + zz) * RING + yy) * 2 + cc
 
@@ -76,8 +79,10 @@
     dev = {
         "f+": (step_along(0, 1), tp),
         "f-": (step_along(0, -1), tp),
+        "f2": (step_along(0, 2), tp),
         "s+": (step_along(1, 1), tp),
         "s-": (step_along(1, -1), tp),
+        "s2": (step_along(1, 2), tp),
         "z": (slot_of(x, 1 - zh, y, core), tp),
         "c": (slot_of(x, zh, y, 1 - core), tp),
     }
@@ -98,8 +103,8 @@
     prt_load = load(0, prt_hbm, prt_ref)
     wk_load = load(1, wk_hbm, wk_ref)
     wv_load = load(2, wv_hbm, wv_ref)
-    ak_load = load(3, ak_hbm, g.at[0, 0, 0, 0, pl.ds(0, anch)])
-    av_load = load(4, av_hbm, g.at[0, 0, 0, 0, pl.ds(keys, anch)])
+    ak_load = load(3, ak_hbm, g.at[0, pl.ds(0, anch)])
+    av_load = load(4, av_hbm, g.at[0, pl.ds(keys, anch)])
     bod_load = load(5, bod_hbm, bod_ref)
     q_load = load(6, q_hbm, q32)
     w_load = load(7, w_hbm, w)
@@ -111,87 +116,76 @@
     pick = (lax.broadcasted_iota(jnp.int32, (ret, tok), 1) == chosen).astype(F32).astype(BF16)
     wk_load.wait()
     wv_load.wait()
-    g[0, 0, 0, 0, anch:keys, :] = jnp.dot(
+    g[0, anch:keys, :] = jnp.dot(
         pick, wk_ref[...], preferred_element_type=F32
     ).astype(BF16)
-    g[0, 0, 0, 0, keys + anch : 2 * keys, :] = jnp.dot(
+    g[0, keys + anch : 2 * keys, :] = jnp.dot(
         pick, wv_ref[...], preferred_element_type=F32
     ).astype(BF16)
 
-    pending = []
-    count = [0]
+    sent = []
 
     def remote(src, dst, recv, to):
         copy = pltpu.make_async_remote_copy(
             src_ref=src,
             dst_ref=dst,
-            send_sem=gs_sem.at[count[0]],
+            send_sem=gs_sem,
             recv_sem=recv,
             device_id=dev[to],
             device_id_type=MESH,
         )
-        count[0] += 1
         copy.start()
-        pending.append(copy)
+        sent.append(1)
 
     def sem(z, d2, d1):
-        return gr_sem.at[(z * RING + d2) * RING + d1]
+        return gr_sem.at[z * 13 + (12 if d2 == 2 else d1 + (0, 4, 0, 8)[d2])]
 
     def arrived(z, d2, d1):
-        ref = g.at[z, d2, 0, d1]
-        if d2 == 0 and d1 == 2:
-            for h in range(2):
-                r = ref.at[pl.ds(h * half, half)]
-                s = gr_sem.at[32 + z * 2 + h]
-                pltpu.make_async_copy(r, r, s).wait()
-        else:
-            pltpu.make_async_copy(ref, ref, sem(z, d2, d1)).wait()
+        ref = g.at[spot(z, d2, 0, d1)]
+        pltpu.make_async_copy(ref, ref, sem(z, d2, d1)).wait()
 
     def to_partner(z, d2, d1):
         remote(
-            g.at[z, d2, 0, d1],
-            g.at[z, d2, 1, d1],
-            pr_sem.at[(z * RING + d2) * RING + d1],
+            g.at[spot(z, d2, 0, d1)],
+            g.at[spot(z, d2, 1, d1)],
+            pr_sem.at[z * RING + d2],
             "c",
         )
 
-    def second_both(z, d1):
-        remote(g.at[z, 0, 0, d1], g.at[z, 3, 0, d1], sem(z, 3, d1), "s+")
-        remote(g.at[z, 0, 0, d1], g.at[z, 1, 0, d1], sem(z, 1, d1), "s-")
+    def second_all(z, d1):
+        own = g.at[spot(z, 0, 0, d1)]
+        remote(own, g.at[spot(z, 3, 0, d1)], sem(z, 3, d1), "s+")
+        remote(own, g.at[spot(z, 1, 0, d1)], sem(z, 1, d1), "s-")
+        if d1 in DIRECT[z]:
+            remote(own, g.at[spot(z, 2, 0, d1)], sem(z, 2, d1), "s2")
 
     def start_own(z):
-        remote(g.at[z, 0, 0, 0], g.at[z, 0, 0, 3], sem(z, 0, 3), "f+")
-        remote(g.at[z, 0, 0, 0], g.at[z, 0, 0, 1], sem(z, 0, 1), "f-")
-        second_both(z, 0)
-
-    def after_first(z):
-        for d1, to, h in ((3, "f+", 0), (1, "f-", 1)):
-            arrived(z, 0, d1)
-            rows = pl.ds(h * half, half)
-            remote(
-                g.at[z, 0, 0, d1, rows],
-                g.at[z, 0, 0, 2, rows],
-                gr_sem.at[32 + z * 2 + h],
-                to,
-            )
-            second_both(z, d1)
-            to_partner(z, 0, d1)
-
-    def after_first_2(z):
-        arrived(z, 0, 2)
-        second_both(z, 2)
-        to_partner(z, 0, 2)
+        own = g.at[spot(z, 0, 0, 0)]
+        remote(own, g.at[spot(z, 0, 0, 3)], sem(z, 0, 3), "f+")
+        remote(own, g.at[spot(z, 0, 0, 1)], sem(z, 0, 1), "f-")
+        remote(own, g.at[spot(z, 0, 0, 2)], sem(z, 0, 2), "f2")
+        second_all(z, 0)
+        to_partner(z, 0, 0)
+
+    def after_first(z, d1):
+        arrived(z, 0, d1)
+        second_all(z, d1)
+        to_partner(z, 0, d1)
 
     def after_second(z, d1):
         for d2, to in ((3, "s+"), (1, "s-")):
             arrived(z, d2, d1)
-            if (d2 == 3) == (d1 in (0, 1)):
-                remote(g.at[z, d2, 0, d1], g.at[z, 2, 0, d1], sem(z, 2, d1), to)
+            if d1 not in DIRECT[z] and (d2 == 3) == (d1 in (0, 2)):
+                remote(g.at[spot(z, d2, 0, d1)], g.at[spot(z, 2, 0, d1)], sem(z, 2, d1), to)
             to_partner(z, d2, d1)
 
+    def whole_row(z, d2, s, arrival):
+        r = g.at[pl.ds(spot(z, d2, s, 0), RING)]
+        pltpu.make_async_copy(r, r, arrival).wait()
+
     def after_second_2(z):
+        whole_row(z, 2, 0, sem(z, 2, 0))
         for d1 in range(RING):
-            arrived(z, 2, d1)
             to_partner(z, 2, d1)
 
     scale = (hd**-0.5) * math.log2(math.e)
@@ -237,15 +231,17 @@
             fold(s, slice(i * QB, (i + 1) * QB), tok, True)
             s = later
 
-    def compute(z, d2):
-        for d1 in range(RING):
-            r = g.at[z, d2, 1, d1]
-            pltpu.make_async_copy(r, r, pr_sem.at[(z * RING + d2) * RING + d1]).wait()
-        n = 2 * RING * keys
-        vt[0:hd, 0:n] = g[z, d2, :, :, keys : 2 * keys, :].reshape(n, hd).T
+    def compute(*units):
+        n = len(units) * RING * keys
         bias = []
-        zz = zh if z == 0 else 1 - zh
-        for s in range(2):
+        for k, (z, d2, s) in enumerate(units):
+            if s == 1:
+                whole_row(z, d2, 1, pr_sem.at[z * RING + d2])
+            at_col = k * RING * keys
+            vt[0:hd, at_col : at_col + RING * keys] = (
+                g[spot(z, d2, s, 0) : spot(z, d2, s, 0) + RING, keys : 2 * keys, :].reshape(RING * keys, hd).T
+            )
+            zz = zh if z == 0 else 1 - zh
             cc = core if s == 0 else 1 - core
             for d1 in range(RING):
                 dx = lax.rem(x + (1 - cc) * d1 + cc * d2, RING)
@@ -255,12 +251,18 @@
                 )
 
         def scores(i):
-            k = g[z, d2, :, :, 0:keys, :].reshape(n, hd)
+            k = jnp.concatenate(
+                [
+                    g[spot(z, d2, s, 0) : spot(z, d2, s, 0) + RING, 0:keys, :].reshape(RING * keys, hd)
+                    for z, d2, s in units
+                ],
+                axis=0,
+            )
             s = lax.dot_general(
                 k, qh[i * QB : (i + 1) * QB, :], (((1,), (1,)), ((), ())), preferred_element_type=F32
             )
             parts = []
-            for j in range(2 * RING):
+            for j in range(len(bias)):
                 parts.append(s[j * keys : j * keys + anch])
                 parts.append(s[j * keys + anch : (j + 1) * keys] + bias[j])
             return jnp.concatenate(parts, axis=0)
@@ -272,44 +274,44 @@
             fold(s, slice(i * QB, (i + 1) * QB), n, False)
             s = later
 
-    pl.semaphore_wait(barrier, 9)
+    pl.semaphore_wait(barrier, 11)
+    remote(g.at[spot(0, 0, 0, 0)], g.at[spot(1, 0, 0, 0)], sem(1, 0, 0), "z")
     start_own(0)
-    remote(g.at[0, 0, 0, 0], g.at[1, 0, 0, 0], sem(1, 0, 0), "z")
-    to_partner(0, 0, 0)
 
     q_load.wait()
-    qh32 = q32[...].astype(F32)
-    own[...] = qh32
+    own[...] = q32[...].astype(F32)
     for h in range(heads):
         qh[h * tok : (h + 1) * tok, :] = own[pl.ds(h, tok, stride=heads), :].astype(BF16)
     vt[hd:, :] = jnp.ones((vt.shape[0] - hd, vt.shape[1]), BF16)
     local_pass()
 
-    after_first(0)
+    after_first(0, 3)
+    after_first(0, 1)
     after_second(0, 0)
-    after_first_2(0)
+    after_first(0, 2)
+    arrived(1, 0, 0)
+    start_own(1)
+    compute((0, 0, 0))
     after_second(0, 3)
     after_second(0, 1)
-    compute(0, 0)
-    arrived(1, 0, 0)
-    start_own(1)
-    to_partner(1, 0, 0)
     after_second(0, 2)
-    after_first(1)
+    after_first(1, 3)
+    after_first(1, 1)
+    compute((0, 1, 0), (0, 0, 1))
+    after_second(1, 0)
+    after_first(1, 2)
     after_second_2(0)
-    compute(0, 1)
-    after_second(1, 0)
-    after_first_2(1)
-    compute(0, 3)
+    compute((0, 3, 0), (0, 1, 1))
     after_second(1, 3)
     after_second(1, 1)
-    compute(0, 2)
-    compute(1, 0)
+    compute((1, 0, 0), (0, 3, 1))
     after_second(1, 2)
-    compute(1, 1)
+    compute((0, 2, 0), (1, 0, 1))
+    compute((1, 1, 0), (0, 2, 1))
     after_second_2(1)
-    compute(1, 3)
-    compute(1, 2)
+    compute((1, 3, 0), (1, 1, 1))
+    compute((1, 2, 0), (1, 3, 1))
+    compute((1, 2, 1))
 
     for h in range(heads):
         cols = slice(h * tok, (h + 1) * tok)
@@ -339,7 +341,7 @@
         return pltpu.make_async_remote_copy(
             src_ref=sbuf.at[ph, r],
             dst_ref=rbuf.at[slot, r],
-            send_sem=ts_sem.at[ph * CHUNKS + ck],
+            send_sem=ts_sem,
             recv_sem=tr_sem.at[slot * CHUNKS + ck],
             device_id=(ctx, to),
             device_id_type=MESH,
@@ -404,16 +406,12 @@
 
     lax.fori_loop(0, CHUNKS, finish, 0)
 
-    for copy in pending:
-        copy.wait_send()
-    for ph in range(3):
-        e, to, slot = plan[ph]
-
-        def drain(ck, c, ph=ph, to=to, slot=slot):
-            tp_copy(ph, ck, to, slot).wait_send()
-            return c
-
-        lax.fori_loop(0, CHUNKS, drain, 0)
+    def drain_all():
+        gone = g.at[pl.ds(0, len(sent))]
+        pltpu.make_async_copy(gone, gone, gs_sem).wait()
+        pltpu.make_async_copy(sbuf, sbuf, ts_sem).wait()
+
+    drain_all()
 
 
 def body(
@@ -433,7 +431,6 @@
     feats = dout // lax.axis_size("tp")
     keys = anch + ret
     n = 2 * RING * keys
-    sends = 2 * (4 + 12 + 16) + 1
 
     def run(*refs):
         kernel(*refs, tok=tok, heads=heads)
@@ -448,7 +445,7 @@
             pltpu.VMEM((tok, hd), BF16),
             pltpu.VMEM((ret, passing_rows.shape[0]), jnp.int32),
             pltpu.SMEM(block_of_device.shape, jnp.int32),
-            pltpu.VMEM((HALVES, RING, 2, RING, 2 * keys, hd), BF16),
+            pltpu.VMEM((HALVES * RING * 2 * RING, 2 * keys, hd), BF16),
             pltpu.VMEM((tok * heads, hd), BF16),
             pltpu.VMEM((tok * heads, hd), BF16),
             pltpu.VMEM(out_weight.shape, BF16),
@@ -461,10 +458,10 @@
             pltpu.VMEM((3, feats, tok), BF16),
             pltpu.VMEM((4, feats, tok), BF16),
             pltpu.SemaphoreType.DMA((8,)),
-            pltpu.SemaphoreType.DMA((sends,)),
-            pltpu.SemaphoreType.DMA((36,)),
-            pltpu.SemaphoreType.DMA((32,)),
-            pltpu.SemaphoreType.DMA((3 * CHUNKS,)),
+            pltpu.SemaphoreType.DMA,
+            pltpu.SemaphoreType.DMA((26,)),
+            pltpu.SemaphoreType.DMA((2 * RING,)),
+            pltpu.SemaphoreType.DMA,
             pltpu.SemaphoreType.DMA((4 * CHUNKS,)),
         ],
         compiler_params=pltpu.CompilerParams(

time: 58.4 us -> 49.9 us (0.85)
  Pallas kernels: 57.5 us -> 49 us
    pallas_call x1, Pallas kernels: 57.5 us -> 49 us  [body(): pl.pallas_call(run, out_shape=jax.ShapeDtypeStruct((feats, tok), BF16), i...]
where the time goes in v3:
time: 49.9 us; the launch traced here: 49.7 us
  Pallas kernels  49 us (98%)
  local copies, waits for them, and re-layouts  0.71 us (1%)
    pallas_call x1, Pallas kernels, body(): pl.pallas_call(run, out_shape=jax.ShapeDtypeStruct((feats, tok), BF16), i...  49 us

profile of v3, /device:TPU:1, one launch (start us, length us, event | category | flops | bytes accessed | tf_op | source)
XLA Modules:
  0.0 49.7 jit_solution(3048809580217986292)
XLA Ops:
  0.0 49.0 %layer.1 = bf16[1024,128]{1,0:T(8,128)(2,1)S(1)} custom-call(bf16[128,128]{1,0:T(8,128)(2,1)} %bitcast.7, bf16[128,128]{1,0:T(8,128)(2,1)} %bitcast.8, bf16[64,128]{1,0:T(8,128)(2,1)} %bitcast.9, bf16[64,128]{1,0:T(8,128)(2,1)} %bitcast.10, s32[32,64]{1,0:T(8,128)} %bitcast.11, s32[64]{0:T(128)} %refs_5_.1, bf16[1024,128]{1,0:T(8,128)(2,1)} %bitcast.6, ...), custom_call_target="tpu_custom_call" | custom-call | tf_op jit(solution)/shard_map/layer/pallas_call | solution.py:438
  49.0 0.7 %copy.10 = bf16[1024,128]{1,0:T(8,128)(2,1)} copy(bf16[1024,128]{1,0:T(8,128)(2,1)S(1)} %layer.1) | data formatting | bytes 524288

commit v4 on v3

--- a/solution.py
+++ b/solution.py
@@ -352,9 +352,9 @@
         pltpu.make_async_copy(r, r, tr_sem.at[slot * CHUNKS + ck]).wait()
 
     plan = (
-        (real(pick2(3, 2)), real(pick2(1, 2)), pick2(3, 1)),
-        (real(pick2(2, 0)), real(pick2(2, 0)), pick2(2, 0)),
-        (real(pick2(1, 3)), real(pick2(1, 3)), pick2(0, 1)),
+        (real(pick2(3, 0)), real(pick2(1, 0)), pick2(3, 0)),
+        (real(pick2(2, 3)), real(pick2(1, 3)), pick2(2, 1)),
+        (real(pick2(1, 2)), real(pick2(1, 2)), pick2(0, 1)),
     )
 
     def send_block(ph):
@@ -362,15 +362,15 @@
 
         def one(ck, c):
             r = pl.ds(pl.multiple_of(ck * rows, rows), rows)
-            if ph < 2:
+            if ph == 0:
                 sbuf[ph, r, :] = product(e, ck).astype(BF16)
             else:
                 part[...] = product(e, ck)
 
                 @pl.when(u == 1)
                 def _():
-                    landed(3, ck)
-                    part[...] += rbuf[3, r, :].astype(F32)
+                    landed(4 - ph, ck)
+                    part[...] += rbuf[4 - ph, r, :].astype(F32)
 
                 sbuf[ph, r, :] = part[...].astype(BF16)
             tp_copy(ph, ck, to, slot).start()
@@ -379,7 +379,6 @@
         lax.fori_loop(0, CHUNKS, one, 0)
 
     send_block(0)
-    send_block(1)
 
     def own_part(ck, c):
         r = pl.ds(pl.multiple_of(ck * rows, rows), rows)
@@ -387,15 +386,11 @@
         return c
 
     lax.fori_loop(0, CHUNKS, own_part, 0)
+    send_block(1)
     send_block(2)
 
     def finish(ck, c):
         r = pl.ds(pl.multiple_of(ck * rows, rows), rows)
-
-        @pl.when(u == 1)
-        def _():
-            landed(2, ck)
-            own[r, :] += rbuf[2, r, :].astype(F32)
 
         landed(0, ck)
         landed(1, ck)

time: 49.9 us -> 49 us (0.982)
  the two profiles are of different devices: /device:TPU:1 before, /device:TPU:32 now
where the time goes in v4:
time: 49 us; the launch traced here: 48.8 us
  Pallas kernels  48.1 us (98%)
  local copies, waits for them, and re-layouts  0.71 us (1%)
    pallas_call x1, Pallas kernels, body(): pl.pallas_call(run, out_shape=jax.ShapeDtypeStruct((feats, tok), BF16), i...  48.1 us

profile of v4, /device:TPU:32, one launch (start us, length us, event | category | flops | bytes accessed | tf_op | source)
XLA Modules:
  0.0 48.8 jit_solution(16906083933214723601)
XLA Ops:
  0.0 48.1 %layer.1 = bf16[1024,128]{1,0:T(8,128)(2,1)S(1)} custom-call(bf16[128,128]{1,0:T(8,128)(2,1)} %bitcast.7, bf16[128,128]{1,0:T(8,128)(2,1)} %bitcast.8, bf16[64,128]{1,0:T(8,128)(2,1)} %bitcast.9, bf16[64,128]{1,0:T(8,128)(2,1)} %bitcast.10, s32[32,64]{1,0:T(8,128)} %bitcast.11, s32[64]{0:T(128)} %refs_5_.1, bf16[1024,128]{1,0:T(8,128)(2,1)} %bitcast.6, ...), custom_call_target="tpu_custom_call" | custom-call | tf_op jit(solution)/shard_map/layer/pallas_call | solution.py:433
  48.1 0.7 %copy.10 = bf16[1024,128]{1,0:T(8,128)(2,1)} copy(bf16[1024,128]{1,0:T(8,128)(2,1)S(1)} %layer.1) | data formatting | bytes 524288

commit v5 on v4

--- a/solution.py
+++ b/solution.py
@@ -13,7 +13,6 @@
 F32 = jnp.float32
 BF16 = jnp.bfloat16
 NEG = -1e30
-QB = 512
 CHUNKS = 4
 DIRECT = ((2,), (2,))
 
@@ -57,6 +56,8 @@
     ret = prt_ref.shape[0]
     keys = anch + ret
     hd = ak_hbm.shape[1]
+    part_tok = tok // 2
+    span = part_tok * heads
     ctx = lax.axis_index("ctx")
     tp = lax.axis_index("tp")
     core = lax.rem(ctx, 2)
@@ -211,31 +212,33 @@
 
     def local_pass():
         vt[0:hd, 0:tok] = wv_ref[...].T
-        row = lax.broadcasted_iota(jnp.int32, (tok, QB), 0)
-        col = lax.broadcasted_iota(jnp.int32, (tok, QB), 1)
-        seen = row <= lax.rem(col, tok)
-
-        def scores(i):
+        row = lax.broadcasted_iota(jnp.int32, (tok, span), 0)
+        col = lax.broadcasted_iota(jnp.int32, (tok, span), 1)
+        place = lax.rem(col, part_tok)
+
+        def scores(cols, p):
             s = lax.dot_general(
-                wk_ref[...],
-                qh[i * QB : (i + 1) * QB, :],
-                (((1,), (1,)), ((), ())),
-                preferred_element_type=F32,
+                wk_ref[...], qh[cols, :], (((1,), (1,)), ((), ())), preferred_element_type=F32
             )
-            return jnp.where(seen, s, NEG)
-
-        blocks = tok * heads // QB
-        s = scores(0)
-        for i in range(blocks):
-            later = scores(i + 1) if i + 1 < blocks else None
-            fold(s, slice(i * QB, (i + 1) * QB), tok, True)
-            s = later
-
-    def compute(*units):
+            return jnp.where(row <= place + p * part_tok, s, NEG)
+
+        first, second = slice(0, span), slice(span, 2 * span)
+        s, later = scores(first, 0), scores(second, 1)
+        fold(s, first, tok, True)
+        fold(later, second, tok, True)
+
+    waited = set()
+
+    both = (slice(0, span), slice(span, 2 * span))
+    early = (slice(0, span // 2), slice(span // 2, span))
+    late = (slice(span, 3 * span // 2), slice(3 * span // 2, 2 * span))
+
+    def compute(*units, blocks=both):
         n = len(units) * RING * keys
         bias = []
         for k, (z, d2, s) in enumerate(units):
-            if s == 1:
+            if s == 1 and (z, d2) not in waited:
+                waited.add((z, d2))
                 whole_row(z, d2, 1, pr_sem.at[z * RING + d2])
             at_col = k * RING * keys
             vt[0:hd, at_col : at_col + RING * keys] = (
@@ -250,7 +253,7 @@
                     jnp.where(bod_ref[slot_of(dx, zz, dy, cc)] < own_block, 0.0, NEG).astype(F32)
                 )
 
-        def scores(i):
+        def scores(cols):
             k = jnp.concatenate(
                 [
                     g[spot(z, d2, s, 0) : spot(z, d2, s, 0) + RING, 0:keys, :].reshape(RING * keys, hd)
@@ -259,7 +262,7 @@
                 axis=0,
             )
             s = lax.dot_general(
-                k, qh[i * QB : (i + 1) * QB, :], (((1,), (1,)), ((), ())), preferred_element_type=F32
+                k, qh[cols, :], (((1,), (1,)), ((), ())), preferred_element_type=F32
             )
             parts = []
             for j in range(len(bias)):
@@ -267,11 +270,10 @@
                 parts.append(s[j * keys + anch : (j + 1) * keys] + bias[j])
             return jnp.concatenate(parts, axis=0)
 
-        blocks = tok * heads // QB
-        s = scores(0)
-        for i in range(blocks):
-            later = scores(i + 1) if i + 1 < blocks else None
-            fold(s, slice(i * QB, (i + 1) * QB), n, False)
+        s = scores(blocks[0])
+        for i, cols in enumerate(blocks):
+            later = scores(blocks[i + 1]) if i + 1 < len(blocks) else None
+            fold(s, cols, n, False)
             s = later
 
     pl.semaphore_wait(barrier, 11)
@@ -281,7 +283,10 @@
     q_load.wait()
     own[...] = q32[...].astype(F32)
     for h in range(heads):
-        qh[h * tok : (h + 1) * tok, :] = own[pl.ds(h, tok, stride=heads), :].astype(BF16)
+        of_head = own[pl.ds(h, tok, stride=heads), :].astype(BF16)
+        for p in range(2):
+            row = p * span + h * part_tok
+            qh[row : row + part_tok, :] = of_head[p * part_tok : (p + 1) * part_tok]
     vt[hd:, :] = jnp.ones((vt.shape[0] - hd, vt.shape[1]), BF16)
     local_pass()
 
@@ -307,17 +312,25 @@
     compute((1, 0, 0), (0, 3, 1))
     after_second(1, 2)
     compute((0, 2, 0), (1, 0, 1))
-    compute((1, 1, 0), (0, 2, 1))
+    compute((1, 1, 0), (0, 2, 1), blocks=early)
     after_second_2(1)
-    compute((1, 3, 0), (1, 1, 1))
-    compute((1, 2, 0), (1, 3, 1))
-    compute((1, 2, 1))
-
-    for h in range(heads):
-        cols = slice(h * tok, (h + 1) * tok)
-        at[h * hd : (h + 1) * hd, :] = (
-            acc[0:hd, cols] * (1.0 / acc[hd : hd + 1, cols])
-        ).astype(BF16)
+    compute((1, 3, 0), (1, 1, 1), blocks=early)
+    compute((1, 2, 0), (1, 3, 1), blocks=early)
+    compute((1, 2, 1), blocks=early)
+
+    low = lax.broadcasted_iota(jnp.int32, (hd, 2 * part_tok), 1) < part_tok
+
+    def normalize(p):
+        for h in range(0, heads, 2):
+            cols = slice(p * span + h * part_tok, p * span + (h + 2) * part_tok)
+            pair = acc[0:hd, cols] * (1.0 / acc[hd : hd + 1, cols])
+            turned = pltpu.roll(pair, part_tok, 1)
+            for k, (lo, hi) in enumerate(((pair, turned), (turned, pair))):
+                rows = slice((h + k) * hd, (h + k + 1) * hd)
+                at[p, 0, rows, :] = jnp.where(low, lo, 0.0).astype(BF16)
+                at[p, 1, rows, :] = jnp.where(low, 0.0, hi).astype(BF16)
+
+    normalize(0)
 
     side = tp // 2
     u = (1 - side) * tp + side * (3 - tp)
@@ -332,9 +345,13 @@
     rows = feats // CHUNKS
     w_load.wait()
 
-    def product(e, ck):
-        at_row = pl.multiple_of(e * feats + ck * rows, rows)
-        return jnp.dot(w[pl.ds(at_row, rows), :], at[...], preferred_element_type=F32)
+    def product(e, p, cc):
+        at_row = pl.multiple_of(e * feats + cc * 2 * rows, rows)
+        return jnp.dot(
+            w[pl.ds(at_row, rows), :], at[p, p], preferred_element_type=F32
+        ) + jnp.dot(
+            w[pl.ds(at_row + rows, rows), :], at[p, 1 - p], preferred_element_type=F32
+        )
 
     def tp_copy(ph, ck, to, slot):
         r = pl.ds(pl.multiple_of(ck * rows, rows), rows)
@@ -357,15 +374,18 @@
         (real(pick2(1, 2)), real(pick2(1, 2)), pick2(0, 1)),
     )
 
-    def send_block(ph):
+    per = CHUNKS // 2
+
+    def send_block(ph, p):
         e, to, slot = plan[ph]
 
-        def one(ck, c):
+        def one(cc, c):
+            ck = p * per + cc
             r = pl.ds(pl.multiple_of(ck * rows, rows), rows)
             if ph == 0:
-                sbuf[ph, r, :] = product(e, ck).astype(BF16)
+                sbuf[ph, r, :] = product(e, p, cc).astype(BF16)
             else:
-                part[...] = product(e, ck)
+                part[...] = product(e, p, cc)
 
                 @pl.when(u == 1)
                 def _():
@@ -376,30 +396,51 @@
             tp_copy(ph, ck, to, slot).start()
             return c
 
-        lax.fori_loop(0, CHUNKS, one, 0)
-
-    send_block(0)
-
-    def own_part(ck, c):
-        r = pl.ds(pl.multiple_of(ck * rows, rows), rows)
-        own[r, :] = product(tp, ck)
-        return c
-
-    lax.fori_loop(0, CHUNKS, own_part, 0)
-    send_block(1)
-    send_block(2)
-
-    def finish(ck, c):
+        lax.fori_loop(0, per, one, 0)
+
+    def own_part(p):
+        def one(cc, c):
+            r = pl.ds(pl.multiple_of((p * per + cc) * rows, rows), rows)
+            own[r, :] = product(tp, p, cc)
+            return c
+
+        lax.fori_loop(0, per, one, 0)
+
+    send_block(0, 0)
+    pl.when(u == 0)(lambda: send_block(1, 0))
+    compute((1, 1, 0), (0, 2, 1), (1, 3, 0), (1, 1, 1), blocks=late)
+    compute((1, 2, 0), (1, 3, 1), (1, 2, 1), blocks=late)
+    normalize(1)
+    send_block(0, 1)
+    own_part(0)
+    pl.when(u == 1)(lambda: send_block(1, 0))
+    own_part(1)
+    send_block(1, 1)
+    send_block(2, 0)
+    send_block(2, 1)
+
+    first_half = lax.broadcasted_iota(jnp.int32, (rows, tok), 1) < part_tok
+
+    def summed(ck):
         r = pl.ds(pl.multiple_of(ck * rows, rows), rows)
 
         landed(0, ck)
         landed(1, ck)
-        out_ref[r, :] = (
-            own[r, :] + rbuf[0, r, :].astype(F32) + rbuf[1, r, :].astype(F32)
-        ).astype(BF16)
-        return c
-
-    lax.fori_loop(0, CHUNKS, finish, 0)
+        return own[r, :] + rbuf[0, r, :].astype(F32) + rbuf[1, r, :].astype(F32)
+
+    def finish():
+        def one(cc, c):
+            here, there = summed(cc), summed(per + cc)
+            r = pl.multiple_of(cc * 2 * rows, rows)
+            out_ref[pl.ds(r, rows), :] = jnp.where(first_half, here, there).astype(BF16)
+            out_ref[pl.ds(r + rows, rows), :] = pltpu.roll(
+                jnp.where(first_half, there, here), part_tok, 1
+            ).astype(BF16)
+            return c
+
+        lax.fori_loop(0, per, one, 0)
+
+    finish()
 
     def drain_all():
         gone = g.at[pl.ds(0, len(sent))]
@@ -425,7 +466,7 @@
     dout = out_weight.shape[0]
     feats = dout // lax.axis_size("tp")
     keys = anch + ret
-    n = 2 * RING * keys
+    n = 4 * RING * keys
 
     def run(*refs):
         kernel(*refs, tok=tok, heads=heads)
@@ -447,7 +488,7 @@
             pltpu.VMEM((8, tok * heads), F32),
             pltpu.VMEM((hd + 16, tok * heads), F32),
             pltpu.VMEM((hd + 16, n), BF16),
-            pltpu.VMEM((heads * hd, tok), BF16),
+            pltpu.VMEM((2, 2, heads * hd, tok), BF16),
             pltpu.VMEM((feats, tok), F32),
             pltpu.VMEM((feats // CHUNKS, tok), F32),
             pltpu.VMEM((3, feats, tok), BF16),

time: 49 us -> 48.4 us (0.988)
  the two profiles are of different devices: /device:TPU:32 before, /device:TPU:56 now
where the time goes in v5:
time: 48.4 us; the launch traced here: 48.2 us
  Pallas kernels  47.5 us (98%)
  local copies, waits for them, and re-layouts  0.71 us (1%)
    pallas_call x1, Pallas kernels, body(): pl.pallas_call(run, out_shape=jax.ShapeDtypeStruct((feats, tok), BF16), i...  47.5 us

profile of v5, /device:TPU:56, one launch (start us, length us, event | category | flops | bytes accessed | tf_op | source)
XLA Modules:
  0.0 48.2 jit_solution(614565807104765953)
XLA Ops:
  0.0 47.5 %layer.1 = bf16[1024,128]{1,0:T(8,128)(2,1)S(1)} custom-call(bf16[128,128]{1,0:T(8,128)(2,1)} %bitcast.7, bf16[128,128]{1,0:T(8,128)(2,1)} %bitcast.8, bf16[64,128]{1,0:T(8,128)(2,1)} %bitcast.9, bf16[64,128]{1,0:T(8,128)(2,1)} %bitcast.10, s32[32,64]{1,0:T(8,128)} %bitcast.11, s32[64]{0:T(128)} %refs_5_.1, bf16[1024,128]{1,0:T(8,128)(2,1)} %bitcast.6, ...), custom_call_target="tpu_custom_call" | custom-call | tf_op jit(solution)/shard_map/layer/pallas_call | solution.py:474
  47.5 0.7 %copy.10 = bf16[1024,128]{1,0:T(8,128)(2,1)} copy(bf16[1024,128]{1,0:T(8,128)(2,1)S(1)} %layer.1) | data formatting | bytes 524288

commit v6 on v5

--- a/solution.py
+++ b/solution.py
@@ -195,6 +195,9 @@
     bod_load.wait()
     own_block = bod_ref[ctx]
 
+    def twice(k):
+        return jnp.concatenate([k, k], axis=1)
+
     def fold(s, cols, n, first):
         top = jnp.max(s, axis=0, keepdims=True)
         if first:
@@ -202,12 +205,12 @@
         else:
             old = m_ref[0:1, cols]
             new = jnp.maximum(old, top)
-        p = jnp.exp2((s - new) * scale).astype(BF16)
+        p = jnp.exp2(s - new).astype(BF16)
         add = jnp.dot(vt[:, 0:n], p, preferred_element_type=F32)
         if first:
             acc[:, cols] = add
         else:
-            acc[:, cols] = acc[:, cols] * jnp.exp2((old - new) * scale) + add
+            acc[:, cols] = acc[:, cols] * jnp.exp2(old - new) + add
         m_ref[0:1, cols] = new
 
     def local_pass():
@@ -218,7 +221,7 @@
 
         def scores(cols, p):
             s = lax.dot_general(
-                wk_ref[...], qh[cols, :], (((1,), (1,)), ((), ())), preferred_element_type=F32
+                twice(wk_ref[...]), qh[cols, :], (((1,), (1,)), ((), ())), preferred_element_type=F32
             )
             return jnp.where(row <= place + p * part_tok, s, NEG)
 
@@ -262,7 +265,7 @@
                 axis=0,
             )
             s = lax.dot_general(
-                k, qh[cols, :], (((1,), (1,)), ((), ())), preferred_element_type=F32
+                twice(k), qh[cols, :], (((1,), (1,)), ((), ())), preferred_element_type=F32
             )
             parts = []
             for j in range(len(bias)):
@@ -283,10 +286,14 @@
     q_load.wait()
     own[...] = q32[...].astype(F32)
     for h in range(heads):
-        of_head = own[pl.ds(h, tok, stride=heads), :].astype(BF16)
+        exact = own[pl.ds(h, tok, stride=heads), :] * scale
+        high = exact.astype(BF16)
+        low_bits = (exact - high.astype(F32)).astype(BF16)
         for p in range(2):
             row = p * span + h * part_tok
-            qh[row : row + part_tok, :] = of_head[p * part_tok : (p + 1) * part_tok]
+            mine = slice(p * part_tok, (p + 1) * part_tok)
+            qh[row : row + part_tok, 0:hd] = high[mine]
+            qh[row : row + part_tok, hd:] = low_bits[mine]
     vt[hd:, :] = jnp.ones((vt.shape[0] - hd, vt.shape[1]), BF16)
     local_pass()
 
@@ -483,7 +490,7 @@
             pltpu.SMEM(block_of_device.shape, jnp.int32),
             pltpu.VMEM((HALVES * RING * 2 * RING, 2 * keys, hd), BF16),
             pltpu.VMEM((tok * heads, hd), BF16),
-            pltpu.VMEM((tok * heads, hd), BF16),
+            pltpu.VMEM((tok * heads, 2 * hd), BF16),
             pltpu.VMEM(out_weight.shape, BF16),
             pltpu.VMEM((8, tok * heads), F32),
             pltpu.VMEM((hd + 16, tok * heads), F32),

time: 48.4 us -> 48.2 us (level)
  no operation moved by 1% of the time
where the time goes in v6:
time: 48.2 us; the launch traced here: 48.1 us
  Pallas kernels  47.4 us (98%)
  local copies, waits for them, and re-layouts  0.71 us (1%)
    pallas_call x1, Pallas kernels, body(): pl.pallas_call(run, out_shape=jax.ShapeDtypeStruct((feats, tok), BF16), i...  47.4 us

profile of v6, /device:TPU:56, one launch (start us, length us, event | category | flops | bytes accessed | tf_op | source)
XLA Modules:
  0.0 48.1 jit_solution(1355913951102743974)
XLA Ops:
  0.0 47.4 %layer.1 = bf16[1024,128]{1,0:T(8,128)(2,1)S(1)} custom-call(bf16[128,128]{1,0:T(8,128)(2,1)} %bitcast.7, bf16[128,128]{1,0:T(8,128)(2,1)} %bitcast.8, bf16[64,128]{1,0:T(8,128)(2,1)} %bitcast.9, bf16[64,128]{1,0:T(8,128)(2,1)} %bitcast.10, s32[32,64]{1,0:T(8,128)} %bitcast.11, s32[64]{0:T(128)} %refs_5_.1, bf16[1024,128]{1,0:T(8,128)(2,1)} %bitcast.6, ...), custom_call_target="tpu_custom_call" | custom-call | tf_op jit(solution)/shard_map/layer/pallas_call | solution.py:481
  47.4 0.7 %copy.10 = bf16[1024,128]{1,0:T(8,128)(2,1)} copy(bf16[1024,128]{1,0:T(8,128)(2,1)S(1)} %layer.1) | data formatting | bytes 524288
